TPU v7x, 32 devices: a whole 2x2x4 slice. The times are simulated.
32 devices in a mesh: zero: 8 (over z, y), width: 4 (over x, core).
Axes of the slice: x: 2, y: 2, z: 4, core: 2. Of those that a mesh axis runs over, the one named last changes fastest.
Arguments:
- train_query: float32 [7168, 7168], P('zero', 'width'), may hold values from -0.09375 to 0.09375
- slow_query: float32 [7168, 7168], P('zero', 'width'), may hold values from -0.0625 to 0.0625
- train_key: float32 [7168, 1024], P('zero', 'width'), may hold values from -0.09375 to 0.09375
- slow_key: float32 [7168, 1024], P('zero', 'width'), may hold values from -0.0625 to 0.0625
- train_value: float32 [7168, 1024], P('zero', 'width'), may hold values from -0.09375 to 0.09375
- slow_value: float32 [7168, 1024], P('zero', 'width'), may hold values from -0.0625 to 0.0625
- norm_train: float32 [7168], P(('zero', 'width')), may hold values from 0.25 to 1.75
- norm_step: float32 [7168], P(('zero', 'width')), may hold values from -0.3 to 0.3
Outputs:
- ready_query: bfloat16 [7168, 7168], P(None, 'width')
- ready_key: bfloat16 [7168, 1024], P(None, 'width')
- ready_value: bfloat16 [7168, 1024], P(None, 'width')
- scale_query: float32 [7168], P('width')
- scale_key: float32 [1024], P('width')
- scale_value: float32 [1024], P('width')
- serve_norm: bfloat16 [7168], replicated
- latest_query: float32 [7168, 7168], P('zero', 'width')
- latest_key: float32 [7168, 1024], P('zero', 'width')
- latest_value: float32 [7168, 1024], P('zero', 'width')
All inputs are finite; a program needn't handle non-finite values.
Results may differ from a plain program's by a relative error of at most 0.0004.
Values may be sent and summed in bfloat16 or wider, within the bound.
A program may use at most 128 MiB of HBM per device.

v0:
```python
import jax
import jax.numpy as jnp
from jax import lax
from jax.sharding import PartitionSpec as P

keep_rate = 0.5


def body(
    train_query, slow_query, train_key, slow_key, train_value, slow_value, norm_train, norm_step
):
    latest_query = keep_rate * slow_query + (1.0 - keep_rate) * train_query
    latest_key = keep_rate * slow_key + (1.0 - keep_rate) * train_key
    latest_value = keep_rate * slow_value + (1.0 - keep_rate) * train_value
    total_query, total_key, total_value = lax.psum(
        (
            jnp.sum(latest_query * latest_query, axis=0),
            jnp.sum(latest_key * latest_key, axis=0),
            jnp.sum(latest_value * latest_value, axis=0),
        ),
        "zero",
    )
    scale_query = jnp.sqrt(total_query)
    scale_key = jnp.sqrt(total_key)
    scale_value = jnp.sqrt(total_value)
    narrow_query, narrow_key, narrow_value = (
        (latest_query / scale_query).astype(jnp.bfloat16),
        (latest_key / scale_key).astype(jnp.bfloat16),
        (latest_value / scale_value).astype(jnp.bfloat16),
    )
    ready_query, ready_key, ready_value = (
        lax.all_gather(narrow_query, "zero", axis=0, tiled=True),
        lax.all_gather(narrow_key, "zero", axis=0, tiled=True),
        lax.all_gather(narrow_value, "zero", axis=0, tiled=True),
    )
    serve_norm = lax.all_gather(
        (norm_train + norm_step).astype(jnp.bfloat16), ("zero", "width"), axis=0, tiled=True
    )
    return (
        ready_query,
        ready_key,
        ready_value,
        scale_query,
        scale_key,
        scale_value,
        serve_norm,
        latest_query,
        latest_key,
        latest_value,
    )


def solution(mesh):
    in_specs = (
        P("zero", "width"),
        P("zero", "width"),
        P("zero", "width"),
        P("zero", "width"),
        P("zero", "width"),
        P("zero", "width"),
        P(("zero", "width")),
        P(("zero", "width")),
    )
    out_specs = (
        P(None, "width"),
        P(None, "width"),
        P(None, "width"),
        P("width"),
        P("width"),
        P("width"),
        P(),
        P("zero", "width"),
        P("zero", "width"),
        P("zero", "width"),
    )
    return jax.shard_map(body, mesh=mesh, in_specs=in_specs, out_specs=out_specs, check_vma=False)
```

profile of v0, /device:TPU:0, one launch (start us, length us, event | category | flops | bytes accessed | tf_op | source)
XLA Modules:
  0.0 712.0 jit_solution(206388412903198558)
XLA Ops:
  7.2 0.0 all-gather.6.cloned.1.call-start
  7.3 8.5 %multiply_reduce_fusion = (f32[1792]{0:T(1024)S(1)}, f32[896,1792]{1,0:T(8,128)}) fusion(f32[896,1792]{1,0:T(8,128)} %param.9, f32[896,1792]{1,0:T(8,128)} %param.8), kind=kLoop, calls=%fused_computation.1 | loop fusion | flops 6420736 | bytes 19274752 | tf_op jit(solution)/shard_map/reduce_sum | solution.py:17
  15.8 0.3 multiply_reduce_fusion.1
  16.0 0.0 copy-start.2
  16.0 0.0 copy-start.3
  16.1 38.9 %all-reduce.1 = (f32[1792]{0:T(1024)S(1)}, f32[256]{0:T(256)S(1)}, f32[256]{0:T(256)S(1)}) all-reduce(f32[1792]{0:T(1024)S(1)} %get-tuple-element.17, f32[256]{0:T(256)S(1)} %get-tuple-element.19, f32[256]{0:T(256)S(1)} %get-tuple-element.13), channel_id=1, replica_groups=mesh['zero'=8,'width'=4] {'zero'}, use_global_device_ids=true, to_apply=%region_1.0 | all-reduce | flops 2304 | bytes 18432 | tf_op jit(solution)/shard_map/psum | solution.py:15
  54.9 0.8 divide_convert_fusion.2
  55.8 0.0 all-gather.6.cloned.1.call-update
  55.8 0.0 all-gather.8.cloned.1.call-start
  55.9 0.8 divide_convert_fusion.1
  56.7 0.0 all-gather.8.cloned.1.call-update
  56.7 0.0 all-gather.4.cloned.1.call-start
  56.8 0.0 copy-start.8
  56.8 5.0 divide_convert_fusion
  61.9 0.0 all-gather.4.cloned.1.call-update
  61.9 0.2 dynamic-update-slice
  62.2 39.7 %all-reduce = bf16[7168]{0:T(1024)(128)(2,1)} all-reduce(bf16[7168]{0:T(1024)(128)(2,1)S(1)} %dynamic-update-slice), channel_id=1, replica_groups=mesh['zero'=8,'width'=4] {'zero','width'}, use_global_device_ids=true, to_apply=%add | all-reduce | flops 7168 | bytes 28672
  101.9 18.6 %all-gather.6.cloned.1.call-done = bf16[7168,256]{1,0:T(8,128)(2,1)} async-done(((bf16[896,256]{1,0:T(8,128)(2,1)}), bf16[7168,256]{1,0:T(8,128)(2,1)}) %all-gather.6.cloned.1.call-update) | async-done | bytes 3670032 | tf_op jit(solution)/shard_map/all_gather | solution.py:33
  120.5 67.7 %all-gather.8.cloned.1.call-done = bf16[7168,256]{1,0:T(8,128)(2,1)} async-done(((bf16[896,256]{1,0:T(8,128)(2,1)}), bf16[7168,256]{1,0:T(8,128)(2,1)}) %all-gather.8.cloned.1.call-update) | async-done | bytes 3670032 | tf_op jit(solution)/shard_map/all_gather | solution.py:34
  188.2 491.1 %all-gather.4.cloned.1.call-done = bf16[7168,1792]{1,0:T(8,128)(2,1)} async-done(((bf16[896,1792]{1,0:T(8,128)(2,1)}), bf16[7168,1792]{1,0:T(8,128)(2,1)}) %all-gather.4.cloned.1.call-update) | async-done | bytes 25690128 | tf_op jit(solution)/shard_map/all_gather | solution.py:32
  679.2 21.0 %copy.22 = bf16[7168,1792]{1,0:T(8,128)(2,1)} copy(bf16[7168,1792]{1,0:T(8,128)(2,1)} %all-gather.4.cloned.1.call-done) | data formatting | bytes 51380224
  700.3 1.9 copy.23
  702.2 1.5 copy-done.1
  703.7 1.8 copy.24
  (27 shorter events, 0.1 us)
Async XLA Ops:
  7.2 8.6 %copy-start.4 = (f32[896,256]{1,0:T(8,128)S(1)}, f32[896,256]{1,0:T(8,128)}, u32[]{:S(2)}) copy-start(f32[896,256]{1,0:T(8,128)} %param.13) | copy-start | bytes 2752516
  7.2 113.3 %all-gather.6.cloned.1.call-start = ((), (), s32[]{:S(2)}) async-start(), calls=%async_computation.1 | async-start | bytes 4128768 | tf_op jit(solution)/shard_map/all_gather | solution.py:33
  7.2 8.5 %copy-start.5 = (f32[896,256]{1,0:T(8,128)S(1)}, f32[896,256]{1,0:T(8,128)}, u32[]{:S(2)}) copy-start(f32[896,256]{1,0:T(8,128)} %param.12) | copy-start | bytes 2752516
  7.2 8.5 %copy-start.6 = (f32[896,256]{1,0:T(8,128)S(1)}, f32[896,256]{1,0:T(8,128)}, u32[]{:S(2)}) copy-start(f32[896,256]{1,0:T(8,128)} %param.11) | copy-start | bytes 2752516
  7.3 8.5 %copy-start.7 = (f32[896,256]{1,0:T(8,128)S(1)}, f32[896,256]{1,0:T(8,128)}, u32[]{:S(2)}) copy-start(f32[896,256]{1,0:T(8,128)} %param.10) | copy-start | bytes 2752516
  16.0 45.8 %copy-start.2 = (f32[896,256]{1,0:T(8,128)}, f32[896,256]{1,0:T(8,128)S(1)}, u32[]{:S(2)}) copy-start(f32[896,256]{1,0:T(8,128)S(1)} %get-tuple-element.40) | copy-start | bytes 2752516
  16.0 45.8 %copy-start.3 = (f32[896,256]{1,0:T(8,128)}, f32[896,256]{1,0:T(8,128)S(1)}, u32[]{:S(2)}) copy-start(f32[896,256]{1,0:T(8,128)S(1)} %get-tuple-element.39) | copy-start | bytes 2752516
  54.9 6.9 copy-start.9
  55.8 132.4 %all-gather.8.cloned.1.call-start = ((), (), s32[]{:S(2)}) async-start(), calls=%async_computation.2 | async-start | bytes 4128768 | tf_op jit(solution)/shard_map/all_gather | solution.py:34
  55.9 6.0 copy-start.10
  56.7 622.5 %all-gather.4.cloned.1.call-start = ((), (), s32[]{:S(2)}) async-start(), calls=%async_computation | async-start | bytes 28901376 | tf_op jit(solution)/shard_map/all_gather | solution.py:32
  56.8 5.1 copy-start.8
  56.8 5.1 copy-start.11
  56.8 5.1 copy-start.12
  679.2 21.1 %copy-start = (bf16[7168,256]{1,0:T(8,128)(2,1)S(1)}, bf16[7168,256]{1,0:T(8,128)(2,1)}, u32[]{:S(2)}) copy-start(bf16[7168,256]{1,0:T(8,128)(2,1)} %all-gather.6.cloned.1.call-done) | copy-start | bytes 11010052
  700.3 3.4 copy-start.1
Sparse Core Ops, SparseCore 0:
  55.9 64.5 all-gather.5
  123.2 64.9 all-gather.7
  190.3 488.9 all-gather.3
where the time goes:
time: 712 us
  waiting for transfers between devices  577 us (81%)
  blocking collectives  78.6 us (11%)
  local copies, waits for them, and re-layouts  26.6 us (4%)
  other arithmetic  15.4 us (2%)
  between operations  13.9 us (2%)
    all_gather x1, waiting for transfers between devices, body(): lax.all_gather(narrow_query, 'zero', axis=0, tiled=True)  491 us
    all_gather x1, waiting for transfers between devices, body(): lax.all_gather(narrow_value, 'zero', axis=0, tiled=True)  67.7 us
    unnamed x1, blocking collectives  39.7 us
    psum x1, blocking collectives, body(): lax.psum((jnp.sum(latest_query * latest_query, axis=0), jnp.sum(latest_ke...  38.9 us
    unnamed x31, local copies, waits for them, and re-layouts  26.6 us
    all_gather x1, waiting for transfers between devices, body(): lax.all_gather(narrow_key, 'zero', axis=0, tiled=True)  18.6 us
  transfers between devices with their start and end apart: 3, of which 3 were waited for; matrix products, arithmetic and copies ran while one was open for 1% of the time, Pallas kernels for 0%

commit v1 on v0

v1 whole, which is shorter than its diff:
```python
import functools

import jax
import jax.numpy as jnp
from jax import lax
from jax.experimental import pallas as pl
from jax.experimental.pallas import tpu as pltpu
from jax.sharding import PartitionSpec as P

keep_rate = 0.5
MESH = pl.DeviceIdType.MESH


def grid_of(count):
    fast = 1
    while (2 * fast) ** 2 <= count and count % (2 * fast) == 0:
        fast *= 2
    return count // fast, fast


def node_at(place, slow, fast):
    if fast == 1:
        return place
    deep = slow - 1
    back = place // (deep * fast)
    column = place // deep
    step = place % deep
    step = step + (column % 2) * (deep - 1 - 2 * step)
    z = (1 - back) * (1 + step)
    y = (1 - back) * column + back * (fast - 1 - (place - deep * fast))
    return z * fast + y


def place_of(node, slow, fast):
    if fast == 1:
        return node
    deep = slow - 1
    z, y = node // fast, node % fast
    out = (z + slow - 1) // slow
    step = z - 1
    step = step + (y % 2) * (deep - 1 - 2 * step)
    return out * (y * deep + step) + (1 - out) * (deep * fast + fast - 1 - y)


def average_kernel(tq, sq, tk, sk, tv, sv, lq, lk, lv, part):
    @pl.when(pl.program_id(0) == 0)
    def _():
        part[...] = jnp.zeros_like(part)

    at = 0
    for train, slow, latest in ((tq, sq, lq), (tk, sk, lk), (tv, sv, lv)):
        value = keep_rate * slow[...] + (1.0 - keep_rate) * train[...]
        latest[...] = value
        wide = value.shape[1]
        part[:, at : at + wide] += jnp.sum(value * value, axis=0, keepdims=True)
        at += wide


def average(arrays):
    rows = arrays[0].shape[0]
    tile = 112 if rows % 112 == 0 else 16
    wides = [a.shape[1] for a in arrays[::2]]

    def spec(wide):
        return pl.BlockSpec((tile, wide), lambda i: (i, 0))

    return pl.pallas_call(
        average_kernel,
        grid=(rows // tile,),
        in_specs=[spec(a.shape[1]) for a in arrays],
        out_specs=[spec(w) for w in wides] + [pl.BlockSpec((1, sum(wides)), lambda i: (0, 0))],
        out_shape=[jax.ShapeDtypeStruct((rows, w), jnp.float32) for w in wides]
        + [jax.ShapeDtypeStruct((1, sum(wides)), jnp.float32)],
        compiler_params=pltpu.CompilerParams(dimension_semantics=("arbitrary",)),
    )(*arrays)


def gather_kernel(
    count, across, cuts, wides, half,
    lq, lk, lv, part, norm_train, norm_step,
    rq, rk, rv, scale_q, scale_k, scale_v, norm_all,
    wq, wk, wv, nq, nk, nv, stats, scale,
    load_sem, keep_sem, stat_send, stat_recv, near_send, near_recv, far_send, far_recv,
    send_sem, recv_sem,
):
    me, side = lax.axis_index("zero"), lax.axis_index("width")
    slow, fast = grid_of(count)
    place = place_of(me, slow, fast)
    ahead = node_at(lax.rem(place + 1, count), slow, fast)
    behind = node_at(lax.rem(place + count - 1, count), slow, fast)
    rows = 2 * half
    latest, wide_in, narrow, ready = (lq, lk, lv), (wq, wk, wv), (nq, nk, nv), (rq, rk, rv)
    pieces = [(0, c * (half // cuts), half // cuts) for c in range(cuts)]
    pieces += [(1, 0, half), (2, 0, half)]

    loads = {}
    for i, (which, first, size) in enumerate(pieces):
        for way in range(2):
            at = pl.ds(way * half + first, size)
            loads[i, way] = pltpu.make_async_copy(
                latest[which].at[at], wide_in[which].at[at], load_sem.at[way, i]
            )
            loads[i, way].start()

    barrier = pltpu.get_barrier_semaphore()
    for k in range(1, count):
        pl.semaphore_signal(
            barrier, inc=1, device_id=(lax.rem(me + k, count), side), device_id_type=MESH
        )
    for k in range(1, across):
        pl.semaphore_signal(
            barrier, inc=1, device_id=(me, lax.rem(side + k, across)), device_id_type=MESH
        )
    stats[me] = part[...]
    mine = me * across + side
    norm_all[mine] = norm_train[...] + norm_step[...]
    pl.semaphore_wait(barrier, count + across - 2)

    def stat_copy(k):
        return pltpu.make_async_remote_copy(
            src_ref=stats.at[me], dst_ref=stats.at[me],
            send_sem=stat_send.at[k - 1], recv_sem=stat_recv.at[k - 1],
            device_id=(lax.rem(me + k, count), side), device_id_type=MESH,
        )

    def near_copy(k):
        return pltpu.make_async_remote_copy(
            src_ref=norm_all.at[mine], dst_ref=norm_all.at[mine],
            send_sem=near_send.at[k - 1], recv_sem=near_recv.at[k - 1],
            device_id=(me, lax.rem(side + k, across)), device_id_type=MESH,
        )

    def far_copy(k):
        at = pl.ds(me * across, across)
        return pltpu.make_async_remote_copy(
            src_ref=norm_all.at[at], dst_ref=norm_all.at[at],
            send_sem=far_send.at[k - 1], recv_sem=far_recv.at[k - 1],
            device_id=(lax.rem(me + k, count), side), device_id_type=MESH,
        )

    for k in range(1, count):
        stat_copy(k).start()
    for k in range(1, across):
        near_copy(k).start()
    for k in range(1, count):
        stat_copy(k).wait_recv()
    total = stats[0]
    for k in range(1, count):
        total = total + stats[k]
    scale[...] = jnp.sqrt(total)
    at = [0, wides[0], wides[0] + wides[1], sum(wides)]
    for i, out in enumerate((scale_q, scale_k, scale_v)):
        out[...] = scale[:, at[i] : at[i + 1]]

    def ring_copy(step, i, way):
        which, first, size = pieces[i]
        shift = step if way else count - step
        owner = node_at(lax.rem(place + shift, count), slow, fast)
        spot = pl.ds(pl.multiple_of(owner * rows + way * half + first, 16), size)
        if isinstance(step, int) and step == 0:
            source = narrow[which].at[pl.ds(way * half + first, size)]
        else:
            source = ready[which].at[spot]
        return pltpu.make_async_remote_copy(
            src_ref=source, dst_ref=ready[which].at[spot],
            send_sem=send_sem.at[way, step, i], recv_sem=recv_sem.at[way, step, i],
            device_id=(behind if way else ahead, side), device_id_type=MESH,
        )

    def arrival(step, i, way):
        which, first, size = pieces[i]
        shift = step + 1 if way else count - step - 1
        owner = node_at(lax.rem(place + shift, count), slow, fast)
        spot = pl.ds(pl.multiple_of(owner * rows + way * half + first, 16), size)
        return pltpu.make_async_remote_copy(
            src_ref=ready[which].at[spot], dst_ref=ready[which].at[spot],
            send_sem=send_sem.at[way, step, i], recv_sem=recv_sem.at[way, step, i],
            device_id=(behind if way else ahead, side), device_id_type=MESH,
        )

    keeps = []
    for i, (which, first, size) in enumerate(pieces):
        for way in range(2):
            spot = pl.ds(way * half + first, size)
            loads[i, way].wait()
            narrow[which][spot, :] = (
                wide_in[which][spot, :] / scale[:, at[which] : at[which + 1]]
            ).astype(jnp.bfloat16)
            ring_copy(0, i, way).start()
            home = pl.ds(pl.multiple_of(me * rows + way * half + first, 16), size)
            keep = pltpu.make_async_copy(
                narrow[which].at[spot], ready[which].at[home], keep_sem.at[way, i]
            )
            keep.start()
            keeps.append(keep)

    for k in range(1, across):
        near_copy(k).wait_recv()
    for k in range(1, count):
        far_copy(k).start()

    def forward(step, carry):
        for i in range(len(pieces)):
            for way in range(2):
                arrival(step - 1, i, way).wait_recv()
                ring_copy(step, i, way).start()
        return carry

    lax.fori_loop(1, count - 1, forward, 0)
    for i in range(len(pieces)):
        for way in range(2):
            arrival(count - 2, i, way).wait_recv()

    def drain(step, carry):
        for i in range(len(pieces)):
            for way in range(2):
                arrival(step, i, way).wait_send()
        return carry

    lax.fori_loop(0, count - 1, drain, 0)
    for keep in keeps:
        keep.wait()
    for k in range(1, count):
        stat_copy(k).wait_send()
        far_copy(k).wait()
    for k in range(1, across):
        near_copy(k).wait_send()


def gather(latest, part, norm_train, norm_step, count, across):
    rows = latest[0].shape[0]
    wides = [a.shape[1] for a in latest]
    half = rows // 2
    cuts = next(c for c in (4, 2, 1) if half % (16 * c) == 0)
    n = cuts + 2
    piece = norm_train.shape[0]
    hbm = pl.BlockSpec(memory_space=pl.ANY)
    vmem = pl.BlockSpec(memory_space=pltpu.VMEM)
    dma = pltpu.SemaphoreType.DMA
    outs = pl.pallas_call(
        functools.partial(gather_kernel, count, across, cuts, wides, half),
        in_specs=[hbm] * 3 + [vmem] * 3,
        out_specs=[hbm] * 3 + [vmem] * 4,
        out_shape=[jax.ShapeDtypeStruct((count * rows, w), jnp.bfloat16) for w in wides]
        + [jax.ShapeDtypeStruct((1, w), jnp.float32) for w in wides]
        + [jax.ShapeDtypeStruct((count * across, 1, piece), jnp.float32)],
        scratch_shapes=[pltpu.VMEM((rows, w), jnp.float32) for w in wides]
        + [pltpu.VMEM((rows, w), jnp.bfloat16) for w in wides]
        + [
            pltpu.VMEM((count, 1, sum(wides)), jnp.float32),
            pltpu.VMEM((1, sum(wides)), jnp.float32),
            dma((2, n)),
            dma((2, n)),
            dma((count - 1,)),
            dma((count - 1,)),
            dma((across - 1,)),
            dma((across - 1,)),
            dma((count - 1,)),
            dma((count - 1,)),
            dma((2, count - 1, n)),
            dma((2, count - 1, n)),
        ],
        compiler_params=pltpu.CompilerParams(collective_id=0, has_side_effects=True),
    )(*latest, part, norm_train.reshape(1, piece), norm_step.reshape(1, piece))
    return outs


def solution(mesh):
    count, across = mesh.shape["zero"], mesh.shape["width"]

    def body(
        train_query, slow_query, train_key, slow_key, train_value, slow_value, norm_train, norm_step
    ):
        *latest, part = average(
            (train_query, slow_query, train_key, slow_key, train_value, slow_value)
        )
        rq, rk, rv, sq, sk, sv, norm = gather(latest, part, norm_train, norm_step, count, across)
        serve_norm = norm.astype(jnp.bfloat16).reshape(-1)
        return (rq, rk, rv, sq.reshape(-1), sk.reshape(-1), sv.reshape(-1), serve_norm, *latest)

    in_specs = (P("zero", "width"),) * 6 + (P(("zero", "width")),) * 2
    out_specs = (
        (P(None, "width"),) * 3 + (P("width"),) * 3 + (P(),) + (P("zero", "width"),) * 3
    )
    return jax.shard_map(body, mesh=mesh, in_specs=in_specs, out_specs=out_specs, check_vma=False)
```

time: 712 us -> 366 us (0.51)
  waiting for transfers between devices: 577 us -> 0 us
  Pallas kernels: 0 us -> 335 us
  blocking collectives: 78.6 us -> 0 us
  other arithmetic: 15.4 us -> 2.16 us
  between operations: 13.9 us -> 0.67 us
    all_gather x3 -> x0, waiting for transfers between devices: 577 us -> none  [the longest x1 491 us: body(): lax.all_gather(narrow_query, 'zero', axis=0, tiled=True)]
    pallas_call x0 -> x2, Pallas kernels: none -> 335 us  [the longest x1 324 us: gather(): pl.pallas_call(functools.partial(gather_kernel, count, across, cuts, wide...]
    unnamed x1 -> x0, blocking collectives: 39.7 us -> none
    psum x1 -> x0, blocking collectives: 38.9 us -> none  [body(): lax.psum((jnp.sum(latest_query * latest_query, axis=0), jnp.sum(latest_ke...]
    reduce_sum x2 -> x0, other arithmetic: 8.75 us -> none  [the longest x1 8.48 us: body(): jnp.sum(latest_query * latest_query, axis=0)]
    unnamed x31 -> x13, local copies, waits for them, and re-layouts: 26.6 us -> 27.4 us
  transfers between devices with their start and end apart: 3 -> 0, of which waited for: 3 -> 0; matrix products, arithmetic and copies ran while one was open for 1% -> 0% of each run, Pallas kernels for 0% -> 0%
where the time goes in v1:
time: 366 us
  Pallas kernels  335 us (92%)
  local copies, waits for them, and re-layouts  28.1 us (8%)
    pallas_call x1, Pallas kernels, gather(): pl.pallas_call(functools.partial(gather_kernel, count, across, cuts, wide...  324 us
    unnamed x13, local copies, waits for them, and re-layouts  27.4 us
    pallas_call x1, Pallas kernels, average(): pl.pallas_call(average_kernel, grid=(rows // tile,), in_specs=[spec(a.sha...  10.6 us

profile of v1, /device:TPU:0, one launch (start us, length us, event | category | flops | bytes accessed | tf_op | source)
XLA Modules:
  0.0 365.6 jit_solution(3546996001203010188)
XLA Ops:
  0.6 10.6 %shard_map.159 = (f32[896,1792]{1,0:T(8,128)}, f32[896,256]{1,0:T(8,128)}, f32[896,256]{1,0:T(8,128)}, f32[1,2304]{1,0:T(1,128)}) custom-call(f32[896,1792]{1,0:T(8,128)} %tq.1, f32[896,1792]{1,0:T(8,128)} %sq.1, f32[896,256]{1,0:T(8,128)} %tk.1, f32[896,256]{1,0:T(8,128)} %sk.1, f32[896,256]{1,0:T(8,128)} %tv.1, f32[896,256]{1,0:T(8,128)} %sv.1), custom_call_target="tpu_custom_call" | custom-call | tf_op jit(solution)/shard_map/pallas_call | solution.py:67
  11.2 324.1 %shard_map.160 = (bf16[7168,1792]{1,0:T(8,128)(2,1)}, bf16[7168,256]{1,0:T(8,128)(2,1)}, bf16[7168,256]{1,0:T(8,128)(2,1)}, f32[1,1792]{1,0:T(1,128)}, f32[1,256...) custom-call(f32[896,1792]{1,0:T(8,128)} %get-tuple-element.49.lq, f32[896,256]{1,0:T(8,128)} %get-tuple-element.50.lk, ...), custom_call_target="tpu_custom_call" | custom-call | tf_op jit(solution)/shard_map/pallas_call | solution.py:240
  335.3 1.3 reduce
  336.6 0.8 convert_reduce_fusion
  337.5 0.7 reshape.43
  338.2 0.0 copy-start.1
  338.2 21.0 %copy.23 = bf16[7168,1792]{1,0:T(8,128)(2,1)} copy(bf16[7168,1792]{1,0:T(8,128)(2,1)} %get-tuple-element.42) | data formatting | bytes 51380224
  359.2 0.0 copy-done.1
  359.2 0.0 copy-start
  359.2 0.0 copy-start.3
  359.2 0.0 copy-start.2
  359.3 1.9 copy.24
  361.1 1.5 copy-done
  362.6 1.8 copy.25
  364.4 0.0 copy-done.3
  364.4 0.6 copy.26
  365.0 0.0 copy-done.2
  365.0 0.6 copy.27
Async XLA Ops:
  338.2 21.1 %copy-start.1 = (bf16[7168,256]{1,0:T(8,128)(2,1)S(1)}, bf16[7168,256]{1,0:T(8,128)(2,1)}, u32[]{:S(2)}) copy-start(bf16[7168,256]{1,0:T(8,128)(2,1)} %get-tuple-element.43) | copy-start | bytes 11010052
  359.2 3.4 copy-start
  359.2 5.2 %copy-start.3 = (f32[1,256]{1,0:T(1,128)S(1)}, f32[1,256]{1,0:T(1,128)}, u32[]{:S(2)}) copy-start(f32[1,256]{1,0:T(1,128)} %get-tuple-element.29) | copy-start | bytes 3076
  359.2 5.8 %copy-start.2 = (f32[1,256]{1,0:T(1,128)S(1)}, f32[1,256]{1,0:T(1,128)}, u32[]{:S(2)}) copy-start(f32[1,256]{1,0:T(1,128)} %get-tuple-element.30) | copy-start | bytes 3076

commit v2 on v1

v2 whole, which is shorter than its diff:
```python
import functools

import jax
import jax.numpy as jnp
from jax import lax
from jax.experimental import pallas as pl
from jax.experimental.pallas import tpu as pltpu
from jax.sharding import PartitionSpec as P

keep_rate = 0.5
MESH = pl.DeviceIdType.MESH


def grid_of(count):
    fast = 1
    while (2 * fast) ** 2 <= count and count % (2 * fast) == 0:
        fast *= 2
    return count // fast, fast


def node_at(place, slow, fast):
    if fast == 1:
        return place
    deep = slow - 1
    back = place // (deep * fast)
    column = place // deep
    step = place % deep
    step = step + (column % 2) * (deep - 1 - 2 * step)
    z = (1 - back) * (1 + step)
    y = (1 - back) * column + back * (fast - 1 - (place - deep * fast))
    return z * fast + y


def place_of(node, slow, fast):
    if fast == 1:
        return node
    deep = slow - 1
    z, y = node // fast, node % fast
    out = (z + slow - 1) // slow
    step = z - 1
    step = step + (y % 2) * (deep - 1 - 2 * step)
    return out * (y * deep + step) + (1 - out) * (deep * fast + fast - 1 - y)


def gather_kernel(
    count, across, width, half, tile,
    tq, sq, tk, sk, tv, sv, norm_train, norm_step,
    rq, rk, rv, lq, lk, lv, scale_q, scale_k, scale_v, norm_all,
    itq, isq, itk, isk, itv, isv, stats_a, stats_b,
    load_sem, stat_send, stat_recv, near_send, near_recv, far_send, far_recv,
    send_sem, recv_sem,
):
    me, side = lax.axis_index("zero"), lax.axis_index("width")
    slow, fast = grid_of(count)
    place = place_of(me, slow, fast)
    ahead = node_at(lax.rem(place + 1, count), slow, fast)
    behind = node_at(lax.rem(place + count - 1, count), slow, fast)
    rows = 2 * half
    trains, slows = ((tq, itq), (tk, itk), (tv, itv)), ((sq, isq), (sk, isk), (sv, isv))
    latest, ready, scales = (lq, lk, lv), (rq, rk, rv), (scale_q, scale_k, scale_v)
    groups = [(1, 0), (2, 0)] + [(0, c) for c in range(tq.shape[1] // width)]

    def columns(c):
        return pl.ds(c * width, width)

    loads = []
    for i, (which, c) in enumerate(groups):
        pair = []
        for j, arrays in enumerate((trains, slows)):
            far, near = arrays[which]
            pair.append(
                pltpu.make_async_copy(far.at[:, columns(c)], near.at[:, columns(c)], load_sem.at[j, i])
            )
            pair[-1].start()
        loads.append(pair)

    barrier = pltpu.get_barrier_semaphore()
    for k in range(1, count):
        pl.semaphore_signal(
            barrier, inc=1, device_id=(lax.rem(me + k, count), side), device_id_type=MESH
        )
    for k in range(1, across):
        pl.semaphore_signal(
            barrier, inc=1, device_id=(me, lax.rem(side + k, across)), device_id_type=MESH
        )
    mine = me * across + side
    norm_all[mine] = norm_train[...] + norm_step[...]

    def stat_copy(part, k):
        stats = (stats_a, stats_b)[part]
        return pltpu.make_async_remote_copy(
            src_ref=stats.at[me], dst_ref=stats.at[me],
            send_sem=stat_send.at[part, k - 1], recv_sem=stat_recv.at[part, k - 1],
            device_id=(lax.rem(me + k, count), side), device_id_type=MESH,
        )

    def near_copy(k):
        return pltpu.make_async_remote_copy(
            src_ref=norm_all.at[mine], dst_ref=norm_all.at[mine],
            send_sem=near_send.at[k - 1], recv_sem=near_recv.at[k - 1],
            device_id=(me, lax.rem(side + k, across)), device_id_type=MESH,
        )

    def far_copy(k):
        at = pl.ds(me * across, across)
        return pltpu.make_async_remote_copy(
            src_ref=norm_all.at[at], dst_ref=norm_all.at[at],
            send_sem=far_send.at[k - 1], recv_sem=far_recv.at[k - 1],
            device_id=(lax.rem(me + k, count), side), device_id_type=MESH,
        )

    def average(i, stats, c_out):
        which, c = groups[i]
        for load in loads[i]:
            load.wait()

        def step(t, total):
            at = pl.ds(pl.multiple_of(t * tile, 16), tile)
            value = (
                keep_rate * slows[which][1][at, columns(c)]
                + (1.0 - keep_rate) * trains[which][1][at, columns(c)]
            )
            latest[which][at, columns(c)] = value
            return total + jnp.sum((value * value).reshape(tile // 8, 8, width), axis=0)

        total = lax.fori_loop(0, rows // tile, step, jnp.zeros((8, width), jnp.float32))
        stats[me, :, columns(c_out)] = jnp.sum(total, axis=0, keepdims=True)

    def ring_copy(owner, step, i, way):
        which, c = groups[i]
        spot = pl.ds(pl.multiple_of(owner * rows + way * half, 16), half)
        piece = ready[which].at[spot, columns(c)]
        return pltpu.make_async_remote_copy(
            src_ref=piece, dst_ref=piece,
            send_sem=send_sem.at[way, step, i], recv_sem=recv_sem.at[way, step, i],
            device_id=(behind if way else ahead, side), device_id_type=MESH,
        )

    def owner_of(step, way):
        return node_at(lax.rem(place + (step if way else count - step), count), slow, fast)

    def send_own(i):
        which, c = groups[i]
        scale = scales[which][:, columns(c)]
        for way in range(2):

            def step(t, carry):
                at = pl.multiple_of(way * half + t * tile, 16)
                home = pl.multiple_of(me * rows + at, 16)
                ready[which][pl.ds(home, tile), columns(c)] = (
                    latest[which][pl.ds(at, tile), columns(c)] / scale
                ).astype(jnp.bfloat16)
                return carry

            lax.fori_loop(0, half // tile, step, 0)
            ring_copy(me, 0, i, way).start()

    def finish(part, members):
        stats = (stats_a, stats_b)[part]
        for k in range(1, count):
            stat_copy(part, k).wait_recv()
        total = stats[0]
        for k in range(1, count):
            total = total + stats[k]
        total = jnp.sqrt(total)
        at = 0
        for which in members:
            wide = scales[which].shape[1]
            scales[which][...] = total[:, at : at + wide]
            at += wide

    average(0, stats_a, 0)
    average(1, stats_a, 1)
    pl.semaphore_wait(barrier, count + across - 2)
    for k in range(1, count):
        stat_copy(0, k).start()
    for k in range(1, across):
        near_copy(k).start()
    early = 2 + (len(groups) - 2) // 2 + 1
    for i in range(2, early):
        average(i, stats_b, groups[i][1])
    finish(0, (1, 2))
    send_own(0)
    send_own(1)
    for i in range(early, len(groups)):
        average(i, stats_b, groups[i][1])
    for k in range(1, count):
        stat_copy(1, k).start()
    finish(1, (0,))
    for i in range(2, len(groups)):
        send_own(i)
    for k in range(1, across):
        near_copy(k).wait_recv()
    for k in range(1, count):
        far_copy(k).start()

    def forward(step, carry):
        owners = owner_of(step, 0), owner_of(step, 1)
        for i in range(len(groups)):
            for way in range(2):
                ring_copy(owners[way], step - 1, i, way).wait_recv()
                ring_copy(owners[way], step, i, way).start()
        return carry

    lax.fori_loop(1, count - 1, forward, 0)
    for i in range(len(groups)):
        for way in range(2):
            ring_copy(owner_of(count - 1, way), count - 2, i, way).wait_recv()

    def drain(step, carry):
        for i in range(len(groups)):
            for way in range(2):
                ring_copy(owner_of(step, way), step, i, way).wait_send()
        return carry

    lax.fori_loop(0, count - 1, drain, 0)
    for k in range(1, count):
        stat_copy(0, k).wait_send()
        stat_copy(1, k).wait_send()
        far_copy(k).wait()
    for k in range(1, across):
        near_copy(k).wait_send()


def gather(arrays, norm_train, norm_step, count, across):
    rows = arrays[0].shape[0]
    wides = [a.shape[1] for a in arrays[::2]]
    half = rows // 2
    width = wides[1]
    tile = 112 if half % 112 == 0 else 16
    n = sum(wides) // width
    piece = norm_train.shape[0]
    hbm = pl.BlockSpec(memory_space=pl.ANY)
    vmem = pl.BlockSpec(memory_space=pltpu.VMEM)
    dma = pltpu.SemaphoreType.DMA
    return pl.pallas_call(
        functools.partial(gather_kernel, count, across, width, half, tile),
        in_specs=[hbm] * 6 + [vmem] * 2,
        out_specs=[vmem] * 10,
        out_shape=[pltpu.VMEM((count * rows, w), jnp.bfloat16) for w in wides]
        + [pltpu.VMEM((rows, w), jnp.float32) for w in wides]
        + [pltpu.VMEM((1, w), jnp.float32) for w in wides]
        + [jax.ShapeDtypeStruct((count * across, 1, piece), jnp.float32)],
        scratch_shapes=[pltpu.VMEM(a.shape, jnp.float32) for a in arrays]
        + [
            pltpu.VMEM((count, 1, 2 * width), jnp.float32),
            pltpu.VMEM((count, 1, wides[0]), jnp.float32),
            dma((2, n)),
            dma((2, count - 1)),
            dma((2, count - 1)),
            dma((across - 1,)),
            dma((across - 1,)),
            dma((count - 1,)),
            dma((count - 1,)),
            dma((2, count - 1, n)),
            dma((2, count - 1, n)),
        ],
        compiler_params=pltpu.CompilerParams(
            collective_id=0, has_side_effects=True,
            vmem_limit_bytes=4 * sum(a.size for a in arrays) + 2**21,
        ),
    )(*arrays, norm_train.reshape(1, piece), norm_step.reshape(1, piece))


def store_kernel(cuts, count, *refs):
    wide, thin = count, (len(refs) - 1) // 2 - count
    wide_in, scale_in = refs[:wide], refs[wide : wide + thin]
    wide_out, scale_out = refs[wide + thin : 2 * wide + thin], refs[2 * wide + thin : -1]
    sem = refs[-1]
    copies = []
    for i, (source, target) in enumerate(zip(wide_in, wide_out)):
        size = source.shape[0] // cuts
        for c in range(cuts):
            at = pl.ds(c * size, size)
            copies.append(pltpu.make_async_copy(source.at[at], target.at[at], sem.at[i, c]))
            copies[-1].start()
    for source, target in zip(scale_in, scale_out):
        target[...] = source[0, :]
    for copy in copies:
        copy.wait()


def store(arrays, scales):
    cuts = 8
    hbm = pl.BlockSpec(memory_space=pl.ANY)
    vmem = pl.BlockSpec(memory_space=pltpu.VMEM)
    return pl.pallas_call(
        functools.partial(store_kernel, cuts, len(arrays)),
        in_specs=[vmem] * (len(arrays) + len(scales)),
        out_specs=[hbm] * len(arrays) + [vmem] * len(scales),
        out_shape=[jax.ShapeDtypeStruct(a.shape, a.dtype) for a in arrays]
        + [jax.ShapeDtypeStruct((s.shape[1],), s.dtype) for s in scales],
        scratch_shapes=[pltpu.SemaphoreType.DMA((len(arrays), cuts))],
        compiler_params=pltpu.CompilerParams(vmem_limit_bytes=2**20),
    )(*arrays, *scales)


def solution(mesh):
    count, across = mesh.shape["zero"], mesh.shape["width"]

    def body(
        train_query, slow_query, train_key, slow_key, train_value, slow_value, norm_train, norm_step
    ):
        *arrays, norm = gather(
            (train_query, slow_query, train_key, slow_key, train_value, slow_value),
            norm_train, norm_step, count, across,
        )
        outs = store(arrays[:1], ()) + store(arrays[1:6], arrays[6:])
        serve_norm = norm.astype(jnp.bfloat16).reshape(-1)
        return (*outs[:3], *outs[6:], serve_norm, *outs[3:6])

    in_specs = (P("zero", "width"),) * 6 + (P(("zero", "width")),) * 2
    out_specs = (
        (P(None, "width"),) * 3 + (P("width"),) * 3 + (P(),) + (P("zero", "width"),) * 3
    )
    return jax.shard_map(body, mesh=mesh, in_specs=in_specs, out_specs=out_specs, check_vma=False)
```

time: 366 us -> 354 us (0.967)
  local copies, waits for them, and re-layouts: 28.1 us -> 11.8 us
  Pallas kernels: 335 us -> 341 us
    unnamed x13 -> x14, local copies, waits for them, and re-layouts: 27.4 us -> 11.1 us
    pallas_call x2 -> x3, Pallas kernels: 335 us -> 341 us  [the longest x1 326 us: gather(): pl.pallas_call(functools.partial(gather_kernel, count, across, width, hal...]
where the time goes in v2:
time: 354 us
  Pallas kernels  341 us (96%)
  local copies, waits for them, and re-layouts  11.8 us (3%)
    pallas_call x1, Pallas kernels, gather(): pl.pallas_call(functools.partial(gather_kernel, count, across, width, hal...  326 us
    pallas_call x2, Pallas kernels, store(): pl.pallas_call(functools.partial(store_kernel, cuts, len(arrays)), in_spe...  14.9 us
    unnamed x14, local copies, waits for them, and re-layouts  11.1 us

profile of v2, /device:TPU:0, one launch (start us, length us, event | category | flops | bytes accessed | tf_op | source)
XLA Modules:
  0.0 354.0 jit_solution(16134115585865596253)
XLA Ops:
  0.6 326.5 %shard_map.159 = (bf16[7168,1792]{1,0:T(8,128)(2,1)S(1)}, bf16[7168,256]{1,0:T(8,128)(2,1)S(1)}, bf16[7168,256]{1,0:T(8,128)(2,1)S(1)}, f32[896,1792]{1,0:T(8,12...) custom-call(f32[896,1792]{1,0:T(8,128)} %tq.1, ...), custom_call_target="tpu_custom_call" | custom-call | tf_op jit(solution)/shard_map/pallas_call | solution.py:236
  327.1 0.0 copy-start
  327.1 0.0 copy-start.2
  327.2 0.0 copy-start.4
  327.2 0.0 copy-start.6
  327.2 8.5 %shard_map.160 = bf16[7168,1792]{1,0:T(8,128)(2,1)} custom-call(bf16[7168,1792]{1,0:T(8,128)(2,1)S(1)} %get-tuple-element.28.refs_0_), custom_call_target="tpu_custom_call" | custom-call | tf_op jit(solution)/shard_map/pallas_call | solution.py:287
  335.7 1.9 copy-done
  337.6 1.2 copy-done.2
  338.8 1.1 copy-done.4
  339.9 0.0 copy-done.6
  339.9 0.1 convert_reduce_fusion
  340.0 0.7 reshape.31
  340.7 0.0 copy-start.1
  340.7 2.8 copy-done.1
  343.5 0.0 copy-start.3
  343.5 2.0 copy-done.3
  345.6 0.0 copy-start.5
  345.6 2.0 copy-done.5
  347.6 6.4 %shard_map.161 = (bf16[7168,256]{1,0:T(8,128)(2,1)}, bf16[7168,256]{1,0:T(8,128)(2,1)}, f32[896,1792]{1,0:T(8,128)}, f32[896,256]{1,0:T(8,128)}, f32[896,256]{1,...) custom-call(bf16[7168,256]{1,0:T(8,128)(2,1)S(1)} %copy-done.3, bf16[7168,256]{1,0:T(8,128)(2,1)S(1)} %copy-done.5, ...), custom_call_target="tpu_custom_call" | custom-call | tf_op jit(solution)/shard_map/pallas_call | solution.py:287
Async XLA Ops:
  327.1 10.5 %copy-start = (f32[896,1792]{1,0:T(8,128)}, f32[896,1792]{1,0:T(8,128)S(1)}, u32[]{:S(2)}) copy-start(f32[896,1792]{1,0:T(8,128)S(1)} %get-tuple-element.31.refs_2_) | copy-start | bytes 19267588
  327.1 11.7 %copy-start.2 = (bf16[7168,256]{1,0:T(8,128)(2,1)}, bf16[7168,256]{1,0:T(8,128)(2,1)S(1)}, u32[]{:S(2)}) copy-start(bf16[7168,256]{1,0:T(8,128)(2,1)S(1)} %get-tuple-element.29.refs_0_) | copy-start | bytes 11010052
  327.2 12.8 %copy-start.4 = (bf16[7168,256]{1,0:T(8,128)(2,1)}, bf16[7168,256]{1,0:T(8,128)(2,1)S(1)}, u32[]{:S(2)}) copy-start(bf16[7168,256]{1,0:T(8,128)(2,1)S(1)} %get-tuple-element.30.refs_1_) | copy-start | bytes 11010052
  327.2 12.7 %copy-start.6 = (f32[32,1,224]{2,1,0:T(1,128)S(1)}, f32[32,1,224]{2,1,0:T(1,128)}, u32[]{:S(2)}) copy-start(f32[32,1,224]{2,1,0:T(1,128)} %get-tuple-element.42) | copy-start | bytes 86020
  340.7 2.8 copy-start.1
  343.5 2.0 copy-start.3
  345.6 2.0 copy-start.5
